TPU v7x, 32 devices: a whole 2x2x4 slice. The times are simulated.
32 devices in a mesh: dp: 4 (over y, x), expert: 8 (over z, core).
Axes of the slice: x: 2, y: 2, z: 4, core: 2. Of those that a mesh axis runs over, the one named last changes fastest.
Arguments:
- expert_ids: int32 [1024, 4], P(('dp', 'expert')), may hold values from 0 to 7, all different within a row; in each aligned block of 32 rows (0 to 31, 32 to 63, ...) at most 20 rows name the same one
- expert_home: int32 [8], replicated, may hold values from 0 to 7, each once
- live_tokens: int32 [32], P(('dp', 'expert')), may hold values from 1 to 32, 768 in all
- gate_weights: float32 [1024, 4], P(('dp', 'expert')), may hold values from 0.1 to 1
- output_grad: bfloat16 [1024, 7168], P(('dp', 'expert')), may hold values from -6 to 6
- saved_hidden: bfloat16 [1024, 4, 1024], P(('dp', 'expert')), may hold values from -0.59765625 to 0.59765625
- down_weight: bfloat16 [8, 1024, 7168], P('expert'), may hold values from -0.1875 to 0.1875
- dense_input: bfloat16 [1024, 7168], P(('dp', 'expert')), may hold values from -6 to 6
- latent_grad: bfloat16 [1024, 256], P(('dp', 'expert')), may hold values from -0.1875 to 0.1875
Outputs:
- hidden_grad: bfloat16 [1024, 4, 1024], P(('dp', 'expert'))
- expert_grad: float32 [8, 1024, 7168], P('expert', 'dp')
- dense_grad: float32 [7168, 256], P(('dp', 'expert'))
Inputs may be any that keep to these rules, and one draw needn't show every extreme that they name: `expert_ids`: each row names 4 different experts. Among the rows of one device no expert is named more than 20 times, and on some devices one expert is named exactly 20 times. A permutation: expert e is held at index expert_home[e] of the expert axis, in every dp replica. `live_tokens`: entry i is the number of real tokens at the start of device i, in the order of the joined dp and expert axes; the rest are padding. Some device has all 32 real.
All inputs are finite; a program needn't handle non-finite values.
Results may differ from a plain program's by a relative error of at most 0.008.
Values may be sent and summed in bfloat16 or wider, within the bound.
A program may use at most 192 MiB of HBM per device.

v0:
```python
import jax
import jax.numpy as jnp
from jax import lax
from jax.sharding import PartitionSpec as P


def on_device(
    expert_ids,
    expert_home,
    live_tokens,
    gate_weights,
    output_grad,
    saved_hidden,
    down_weight,
    dense_input,
    latent_grad,
):
    n_group = lax.axis_size("expert")
    tok_rows, top_count = expert_ids.shape
    model_width = output_grad.shape[1]
    hidden_units = saved_hidden.shape[2]
    capacity = tok_rows * top_count * 5 // (4 * n_group)
    is_live = jnp.arange(tok_rows, dtype=jnp.int32) < live_tokens[0]
    masked_grad = jnp.where(is_live[:, None], latent_grad, jnp.zeros_like(latent_grad))
    owned_columns = lax.all_to_all(
        dense_input, ("dp", "expert"), split_axis=1, concat_axis=0, tiled=True
    )
    dense_grad = lax.dot_general(
        owned_columns,
        lax.all_gather(masked_grad, ("dp", "expert"), axis=0, tiled=True),
        (((0,), (0,)), ((), ())),
        preferred_element_type=jnp.float32,
    )
    pair_count = tok_rows * top_count
    flat_ids = expert_ids.reshape(pair_count)
    expert_count = expert_home.shape[0]
    id_table = (flat_ids[:, None] == jnp.arange(expert_count, dtype=jnp.int32)[None, :]).astype(
        jnp.int32
    )
    home_slot = jnp.sum(id_table * expert_home[None, :], axis=1)
    slot_table = (home_slot[:, None] == jnp.arange(n_group, dtype=jnp.int32)[None, :]).astype(
        jnp.int32
    )
    earlier = jnp.cumsum(slot_table, axis=0) - slot_table
    position = jnp.sum(earlier * slot_table, axis=1)
    slot_index = home_slot * capacity + position
    pair_ids = jnp.arange(pair_count, dtype=jnp.int32)
    source_pair = jnp.zeros((n_group * capacity,), jnp.int32).at[slot_index].set(pair_ids)
    filled = jnp.zeros((n_group * capacity,), jnp.bool_).at[slot_index].set(True)
    source_token = source_pair // top_count
    pair_scale = (gate_weights * is_live[:, None].astype(jnp.float32)).reshape(pair_count)
    slot_scale = jnp.where(filled, pair_scale[source_pair], jnp.float32(0.0))
    grad_rows = (output_grad[source_token].astype(jnp.float32) * slot_scale[:, None]).astype(
        jnp.bfloat16
    )
    flat_hidden = saved_hidden.reshape(pair_count, hidden_units)
    hidden_rows = jnp.where(filled[:, None], flat_hidden[source_pair], jnp.zeros((), jnp.bfloat16))
    arrived_grad, arrived_hidden = (
        lax.all_to_all(
            grad_rows.reshape(n_group, capacity, model_width),
            "expert",
            split_axis=0,
            concat_axis=0,
            tiled=True,
        ),
        lax.all_to_all(
            hidden_rows.reshape(n_group, capacity, hidden_units),
            "expert",
            split_axis=0,
            concat_axis=0,
            tiled=True,
        ),
    )
    arrived_grad = arrived_grad.reshape(n_group * capacity, model_width)
    arrived_hidden = arrived_hidden.reshape(n_group * capacity, hidden_units)
    expert_weight = down_weight[0]
    input_grad = lax.dot_general(
        arrived_grad, expert_weight, (((1,), (1,)), ((), ())), preferred_element_type=jnp.float32
    ).astype(jnp.bfloat16)
    returned = lax.all_to_all(
        input_grad.reshape(n_group, capacity, hidden_units),
        "expert",
        split_axis=0,
        concat_axis=0,
        tiled=True,
    )
    expert_grad = lax.psum_scatter(
        lax.dot_general(
            arrived_hidden,
            arrived_grad,
            (((0,), (0,)), ((), ())),
            preferred_element_type=jnp.float32,
        ),
        "dp",
        scatter_dimension=0,
        tiled=True,
    )
    hidden_grad = returned.reshape(n_group * capacity, hidden_units)[slot_index].reshape(
        tok_rows, top_count, hidden_units
    )
    return (hidden_grad, expert_grad[None], dense_grad)


def solution(mesh):
    placed = (
        P(("dp", "expert"), None),
        P(),
        P(("dp", "expert")),
        P(("dp", "expert"), None),
        P(("dp", "expert"), None),
        P(("dp", "expert"), None, None),
        P("expert", None, None),
        P(("dp", "expert"), None),
        P(("dp", "expert"), None),
    )
    return jax.shard_map(
        on_device,
        mesh=mesh,
        in_specs=placed,
        out_specs=(
            P(("dp", "expert"), None, None),
            P("expert", "dp", None),
            P(("dp", "expert"), None),
        ),
        check_vma=False,
    )
```

profile of v0, /device:TPU:0, one launch (start us, length us, event | category | flops | bytes accessed | tf_op | source)
XLA Modules:
  0.0 383.3 jit_solution(13463174959926582914)
XLA Ops:
  7.2 0.0 copy-start
  7.2 0.8 copy.14
  8.0 0.1 eq.28
  8.1 0.8 select_reduce_fusion.1
  8.9 0.1 fusion.5
  9.0 0.2 reduce_window_sum.11
  9.2 0.2 select_reduce_fusion
  9.4 1.0 scatter_custom_fusion
  10.4 1.0 reshape.88
  11.4 0.9 gather_fusion.3
  12.4 0.1 gather.18
  12.5 1.0 scatter_custom_fusion.1
  13.5 0.1 broadcast_in_dim.61
  13.6 0.9 broadcast_select_fusion
  14.4 6.4 %all-to-all-start.2 = ((bf16[8,20,1024]{2,1,0:T(8,128)(2,1)}), bf16[8,20,1024]{2,1,0:T(8,128)(2,1)}, u32[]{:S(2)}, u32[]{:S(2)}) async-start(bf16[8,20,1024]{2,1,0:T(8,128)(2,1)} %broadcast_select_fusion), calls=%async_computation.2 | async-start | bytes 786432 | tf_op jit(solution)/shard_map/all_to_all | solution.py:66
  20.8 0.0 reduce-scatter.2.cloned.1.call-start
  20.8 0.0 copy-done
  20.8 2.0 gather_fusion
  22.9 0.0 copy-start.6
  22.9 2.9 reshape.89
  26.4 0.0 copy-done.6
  26.4 0.1 copy.15
  26.5 0.1 reshape.83
  26.6 1.6 gather_fusion.1
  28.2 0.1 mul.51
  28.3 3.1 multiply_convert_fusion
  31.4 2.1 all-to-all-done.2
  33.4 65.9 %all_to_all.34 = bf16[8,20,7168]{2,1,0:T(8,128)(2,1)S(1)} all-to-all(bf16[8,20,7168]{2,1,0:T(8,128)(2,1)S(1)} %multiply_convert_fusion), channel_id=1, replica_groups=mesh['dp'=4,'expert'=8] {'expert'}, dimensions={0} | all-to-all | bytes 4587520 | tf_op jit(solution)/shard_map/all_to_all | solution.py:59
  99.3 0.0 copy-start.2
  99.3 1.5 copy-done.2
  100.8 12.7 %convolution_bitcast_fusion = f32[1024,7168]{1,0:T(8,128)} fusion(bf16[8,20,1024]{2,1,0:T(8,128)(2,1)} %all-to-all-done.2, bf16[8,20,7168]{2,1,0:T(8,128)(2,1)S(1)} %all_to_all.34), kind=kOutput, calls=%fused_computation.6 | convolution fusion | flops 2348810240 | bytes 31981568 | tf_op jit(solution)/shard_map/dot_general | solution.py:88
  113.5 0.0 copy-start.4
  113.5 0.0 reduce-scatter.2.cloned.1.call-update
  113.5 1.0 copy-done.4
  114.5 0.0 copy-start.5
  114.5 0.0 copy-start.3
  114.5 1.6 all_to_all.26
  116.1 2.1 copy.16
  118.2 3.7 all-to-all-start.3
  121.9 0.0 copy-done.5
  121.9 0.1 broadcast_select_fusion.1
  122.0 0.0 copy-done.3
  122.0 2.1 reshape.84
  124.2 10.9 %fusion.2 = bf16[160,1024]{1,0:T(8,128)(2,1)S(1)} fusion(bf16[160,7168]{1,0:T(8,128)(2,1)} %reshape.84, bf16[1,1024,7168]{2,1,0:T(8,128)(2,1)} %param.15), kind=kOutput, calls=%fused_computation.10 | convolution fusion | flops 2348974080 | bytes 17301504 | tf_op jit(solution)/shard_map/dot_general | solution.py:77
  135.0 0.8 reshape.85
  135.9 2.4 all-to-all-done.3
  138.2 3.5 all-to-all-start.1
  141.7 0.0 copy-start.1
  141.7 45.2 %all_gather.3 = bf16[1024,256]{1,0:T(8,128)(2,1)S(1)} all-gather(bf16[32,256]{1,0:T(8,128)(2,1)S(1)} %broadcast_select_fusion.1), channel_id=1, replica_groups=mesh['dp'=4,'expert'=8] {'dp','expert'}, dimensions={0}, use_global_device_ids=true | all-gather | bytes 540672 | tf_op jit(solution)/shard_map/all_gather | solution.py:30
  186.9 2.1 convolution_bitcast_fusion.1
  189.0 0.0 all-to-all-done.1
  189.0 0.1 reshape.86
  189.1 0.9 gather_fusion.2
  189.9 0.8 reshape.87
  190.7 185.7 %reduce-scatter.2.cloned.1.call-done = f32[256,7168]{1,0:T(8,128)} async-done(((f32[1024,7168]{1,0:T(8,128)}), f32[256,7168]{1,0:T(8,128)}) %reduce-scatter.2.cloned.1.call-update) | async-done | bytes 7340048 | tf_op jit(solution)/shard_map/reduce_scatter | solution.py:87
  376.4 0.0 copy-done.1
  (10 shorter events, 0.1 us)
Async XLA Ops:
  7.2 13.7 %copy-start = (bf16[32,7168]{1,0:T(8,128)(2,1)S(1)}, bf16[32,7168]{1,0:T(8,128)(2,1)}, u32[]{:S(2)}) copy-start(bf16[32,7168]{1,0:T(8,128)(2,1)} %param.13) | copy-start | bytes 1376260
  14.4 19.0 %all-to-all-start.2 = ((bf16[8,20,1024]{2,1,0:T(8,128)(2,1)}), bf16[8,20,1024]{2,1,0:T(8,128)(2,1)}, u32[]{:S(2)}, u32[]{:S(2)}) async-start(bf16[8,20,1024]{2,1,0:T(8,128)(2,1)} %broadcast_select_fusion), calls=%async_computation.2 | async-start | bytes 786432 | tf_op jit(solution)/shard_map/all_to_all | solution.py:66
  20.8 355.6 %reduce-scatter.2.cloned.1.call-start = ((), (), s32[]{:S(2)}) async-start(), calls=%async_computation.5 | async-start | bytes 36700160 | tf_op jit(solution)/shard_map/reduce_scatter | solution.py:87
  22.9 3.6 copy-start.6
  99.3 1.5 copy-start.2
  113.5 1.0 copy-start.4
  114.5 7.4 %copy-start.5 = (bf16[32,256]{1,0:T(8,128)(2,1)S(1)}, bf16[32,256]{1,0:T(8,128)(2,1)}, u32[]{:S(2)}) copy-start(bf16[32,256]{1,0:T(8,128)(2,1)} %param.17) | copy-start | bytes 49156
  114.5 7.5 %copy-start.3 = (bf16[8,20,7168]{2,1,0:T(8,128)(2,1)S(1)}, bf16[8,20,7168]{2,1,0:T(8,128)(2,1)}, u32[]{:S(2)}) copy-start(bf16[8,20,7168]{2,1,0:T(8,128)(2,1)} %copy-done.2) | copy-start | bytes 6881284
  118.2 20.0 %all-to-all-start.3 = ((bf16[32,32,224]{2,0,1:T(8,128)(2,1)}), bf16[32,32,224]{2,0,1:T(8,128)(2,1)}, u32[]{:S(2)}, u32[]{:S(2)}) async-start(bf16[32,32,224]{2,0,1:T(8,128)(2,1)} %copy.16), calls=%async_computation.4 | async-start | bytes 1048576 | tf_op jit(solution)/shard_map/all_to_all | solution.py:25
  138.2 50.8 %all-to-all-start.1 = ((bf16[8,20,1024]{2,1,0:T(8,128)(2,1)}), bf16[8,20,1024]{2,1,0:T(8,128)(2,1)S(1)}, u32[]{:S(2)}, u32[]{:S(2)}) async-start(bf16[8,20,1024]{2,1,0:T(8,128)(2,1)} %reshape.85), calls=%async_computation.1 | async-start | bytes 786432 | tf_op jit(solution)/shard_map/all_to_all | solution.py:80
  141.7 234.7 %copy-start.1 = (bf16[32,7168]{1,0:T(8,128)(2,1)S(1)}, bf16[32,7168]{1,0:T(8,128)(2,1)}, u32[]{:S(2)}) copy-start(bf16[32,7168]{1,0:T(8,128)(2,1)} %param.13) | copy-start | bytes 1376260
Sparse Core Ops, SparseCore 0:
  113.7 262.6 reduce-scatter.1
where the time goes:
time: 384 us; the launch traced here: 383 us
  waiting for transfers between devices  190 us (49%)
  blocking collectives  111 us (29%)
  matrix products  25.6 us (7%)
  local copies, waits for them, and re-layouts  22.7 us (6%)
  between operations  14.9 us (4%)
  starting transfers between devices  13.5 us (4%)
  other arithmetic  5.34 us (1%)
    reduce_scatter x1, waiting for transfers between devices, on_device(): lax.psum_scatter(lax.dot_general(arrived_hidden, arrived_grad, (((0,), (0...  186 us
    all_to_all x1, blocking collectives, on_device(): lax.all_to_all(grad_rows.reshape(n_group, capacity, model_width), 'expert...  65.9 us
    all_gather x1, blocking collectives, on_device(): lax.all_gather(masked_grad, ('dp', 'expert'), axis=0, tiled=True)  45.2 us
    dot_general x1, matrix products, on_device(): lax.dot_general(arrived_hidden, arrived_grad, (((0,), (0,)), ((), ())), p...  12.7 us
    dot_general x1, matrix products, on_device(): lax.dot_general(arrived_grad, expert_weight, (((1,), (1,)), ((), ())), pr...  10.9 us
  transfers between devices with their start and end apart: 4, of which 3 were waited for; matrix products, arithmetic and copies ran while one was open for 8% of the time, Pallas kernels for 0%

commit v1 on v0

v1 whole, which is shorter than its diff:
```python
import jax
import jax.numpy as jnp
from jax import lax
from jax.sharding import PartitionSpec as P

BOTH = ("dp", "expert")


def on_device(
    expert_ids,
    expert_home,
    live_tokens,
    gate_weights,
    output_grad,
    saved_hidden,
    down_weight,
    dense_input,
    latent_grad,
):
    n_dp = lax.axis_size("dp")
    n_group = lax.axis_size("expert")
    tok_rows, top_count = expert_ids.shape
    model_width = output_grad.shape[1]
    hidden_units = saved_hidden.shape[2]
    owned_units = hidden_units // n_dp
    is_live = jnp.arange(tok_rows, dtype=jnp.int32) < live_tokens[0]
    masked_grad = jnp.where(is_live[:, None], latent_grad, jnp.zeros_like(latent_grad))
    everyone = lax.all_gather(
        jnp.concatenate([output_grad, masked_grad], axis=1), BOTH, axis=0, tiled=True
    )
    all_grad = everyone[:, :model_width]
    all_latent = everyone[:, model_width:]
    ids_at = expert_ids[:, :, None] == jnp.arange(expert_home.shape[0], dtype=jnp.int32)
    home = jnp.sum(jnp.where(ids_at, expert_home, 0), axis=2)
    scale = jnp.where(is_live[:, None], gate_weights, 0.0)
    at_slot = home[:, :, None] == jnp.arange(n_group, dtype=jnp.int32)
    slot_scale = jnp.where(at_slot, scale[:, :, None], 0.0)
    hidden = saved_hidden.astype(jnp.float32)
    by_slot = sum(
        slot_scale[:, k].T[:, :, None] * hidden[None, :, k] for k in range(top_count)
    ).astype(jnp.bfloat16)
    by_owner = by_slot.reshape(n_group, tok_rows, n_dp, owned_units).transpose(2, 0, 1, 3)
    by_owner = by_owner.reshape(n_dp * n_group, tok_rows, owned_units)
    dense_cut = dense_input.reshape(tok_rows, n_dp * n_group, -1).transpose(1, 0, 2)
    sent = jnp.concatenate([by_owner, dense_cut], axis=2)
    got = lax.all_to_all(sent, BOTH, split_axis=0, concat_axis=0, tiled=True)
    got = got.reshape(n_dp * n_group * tok_rows, -1)
    my_hidden = got[:, :owned_units]
    my_dense = got[:, owned_units:]
    replica_rows = n_group * tok_rows
    my_replica = lax.dynamic_slice(
        everyone, (lax.axis_index("dp") * replica_rows, 0), (replica_rows, model_width)
    )
    product = lax.dot_general(
        my_replica, down_weight[0], (((1,), (1,)), ((), ())), preferred_element_type=jnp.float32
    ).astype(jnp.bfloat16)
    returned = lax.all_to_all(
        product.reshape(n_group, tok_rows, hidden_units),
        "expert",
        split_axis=0,
        concat_axis=0,
        tiled=True,
    )
    expert_grad = lax.dot_general(
        my_hidden, all_grad, (((0,), (0,)), ((), ())), preferred_element_type=jnp.float32
    )
    dense_grad = lax.dot_general(
        my_dense, all_latent, (((0,), (0,)), ((), ())), preferred_element_type=jnp.float32
    )
    returned = returned.astype(jnp.float32)
    hidden_grad = jnp.stack(
        [
            sum(slot_scale[:, k, s][:, None] * returned[s] for s in range(n_group))
            for k in range(top_count)
        ],
        axis=1,
    ).astype(jnp.bfloat16)
    return (hidden_grad, expert_grad[None], dense_grad)


def solution(mesh):
    placed = (
        P(BOTH, None),
        P(),
        P(BOTH),
        P(BOTH, None),
        P(BOTH, None),
        P(BOTH, None, None),
        P("expert", None, None),
        P(BOTH, None),
        P(BOTH, None),
    )
    return jax.shard_map(
        on_device,
        mesh=mesh,
        in_specs=placed,
        out_specs=(P(BOTH, None, None), P("expert", "dp", None), P(BOTH, None)),
        check_vma=False,
    )
```

time: 384 us -> 172 us (0.45)
  blocking collectives: 111 us -> 0 us
  waiting for transfers between devices: 190 us -> 107 us
  local copies, waits for them, and re-layouts: 22.7 us -> 4.76 us
    reduce_scatter x1 -> x0, waiting for transfers between devices: 186 us -> none  [on_device(): lax.psum_scatter(lax.dot_general(arrived_hidden, arrived_grad, (((0,), (0...]
    all_gather x0 -> x1, waiting for transfers between devices: none -> 107 us  [on_device(): lax.all_gather(jnp.concatenate([output_grad, masked_grad], axis=1), BOTH,...]
    all_to_all x1 -> x0, blocking collectives: 65.9 us -> none  [on_device(): lax.all_to_all(grad_rows.reshape(n_group, capacity, model_width), 'expert...]
    all_gather x1 -> x0, blocking collectives: 45.2 us -> none  [on_device(): lax.all_gather(masked_grad, ('dp', 'expert'), axis=0, tiled=True)]
    gather x5 -> x0, local copies, waits for them, and re-layouts: 5.42 us -> none  [the longest x1 2 us: on_device(): output_grad[source_token].astype(jnp.float32) * slot_scale[:, None]]
    all_to_all x3 -> x2, starting transfers between devices: 13.5 us -> 11 us  [the longest x1 7.33 us: on_device(): got = lax.all_to_all(sent, BOTH, split_axis=0, concat_axis=0, tiled=True)]
  transfers between devices with their start and end apart: 4 -> 3, of which waited for: 3 -> 2; matrix products, arithmetic and copies ran while one was open for 8% -> 20% of each run, Pallas kernels for 0% -> 0%
where the time goes in v1:
time: 172 us; the launch traced here: 171 us
  waiting for transfers between devices  107 us (62%)
  matrix products  25.4 us (15%)
  between operations  14.9 us (9%)
  starting transfers between devices  11 us (6%)
  other arithmetic  7.68 us (4%)
  local copies, waits for them, and re-layouts  4.76 us (3%)
    all_gather x1, waiting for transfers between devices, on_device(): lax.all_gather(jnp.concatenate([output_grad, masked_grad], axis=1), BOTH,...  107 us
    dot_general x1, matrix products, on_device(): lax.dot_general(my_hidden, all_grad, (((0,), (0,)), ((), ())), preferred_...  12.3 us
    dot_general x1, matrix products, on_device(): lax.dot_general(my_replica, down_weight[0], (((1,), (1,)), ((), ())), pre...  11.1 us
    all_to_all x1, starting transfers between devices, on_device(): got = lax.all_to_all(sent, BOTH, split_axis=0, concat_axis=0, tiled=True)  7.33 us
    all_to_all x1, starting transfers between devices, on_device(): lax.all_to_all(product.reshape(n_group, tok_rows, hidden_units), 'expert'...  3.67 us
  transfers between devices with their start and end apart: 3, of which 2 were waited for; matrix products, arithmetic and copies ran while one was open for 20% of the time, Pallas kernels for 0%

profile of v1, /device:TPU:0, one launch (start us, length us, event | category | flops | bytes accessed | tf_op | source)
XLA Modules:
  0.0 171.2 jit_solution(10433014168137700257)
XLA Ops:
  7.2 0.0 all-gather.2.cloned.1.call-start
  7.9 0.8 broadcast_select_fusion
  8.7 1.8 %pad_maximum_fusion.1 = bf16[32,7424]{1,0:T(8,128)(2,1)} fusion(bf16[32,256]{1,0:T(8,128)(2,1)S(1)} %broadcast_select_fusion, bf16[32,7168]{1,0:T(8,128)(2,1)} %param.13), kind=kLoop, calls=%fused_computation.20 | loop fusion | flops 950272 | bytes 950272 | tf_op jit(solution)/shard_map/concatenate | solution.py:29
  10.5 0.0 all-gather.2.cloned.1.call-update
  10.5 1.0 convert_element_type.18
  11.5 1.4 slice_reduce_fusion.3
  12.9 0.1 mul.751
  13.0 0.1 mul.775
  13.2 0.1 mul.767
  13.3 0.1 mul.759
  13.4 1.8 %reshape.1381 = bf16[32,32,224]{2,1,0:T(8,128)(2,1)S(1)} reshape(bf16[32,7168]{1,0:T(8,128)(2,1)} %param.16) | data formatting | bytes 917504 | tf_op jit(solution)/shard_map/reshape | solution.py:44
  15.1 0.3 copy.37
  15.4 0.8 select_reduce_fusion
  16.2 0.7 broadcast_select_fusion.1
  16.9 0.7 fusion.14
  17.7 1.1 pad_maximum_fusion
  18.8 7.3 %all-to-all-start.1 = ((bf16[32,32,480]{2,1,0:T(8,128)(2,1)}), bf16[32,32,480]{2,1,0:T(8,128)(2,1)S(1)}, u32[]{:S(2)}, u32[]{:S(2)}) async-start(bf16[32,32,480]{2,1,0:T(8,128)(2,1)} %pad_maximum_fusion), calls=%async_computation.1 | async-start | bytes 2097152 | tf_op jit(solution)/shard_map/all_to_all | solution.py:46
  26.2 106.7 %all-gather.2.cloned.1.call-done = bf16[1024,7424]{1,0:T(8,128)(2,1)} async-done(((bf16[32,7424]{1,0:T(8,128)(2,1)}), bf16[1024,7424]{1,0:T(8,128)(2,1)}) %all-gather.2.cloned.1.call-update) | async-done | bytes 15204368 | tf_op jit(solution)/shard_map/all_gather | solution.py:28
  132.9 11.1 %fusion.8 = bf16[256,1024]{1,0:T(8,128)(2,1)} fusion(bf16[1,1024,7168]{2,1,0:T(8,128)(2,1)} %param.15, bf16[1024,7424]{1,0:T(8,128)(2,1)} %all-gather.2.cloned.1.call-done, s32[]{:T(128)S(6)} %select_n.23), kind=kOutput, calls=%fused_computation.6 | convolution fusion | flops 3758358528 | bytes 18874372 | tf_op jit(solution)/shard_map/dot_general | solution.py:54
  144.0 0.0 all-to-all-done.1
  144.0 3.7 %all-to-all-start = ((bf16[8,32,1024]{2,1,0:T(8,128)(2,1)}), bf16[8,32,1024]{2,1,0:T(8,128)(2,1)S(1)}, u32[]{:S(2)}, u32[]{:S(2)}) async-start(bf16[8,32,1024]{2,1,0:T(8,128)(2,1)} %bitcast.3), calls=%async_computation | async-start | bytes 1048576 | tf_op jit(solution)/shard_map/all_to_all | solution.py:57
  147.7 2.1 %fusion.17 = f32[224,256]{1,0:T(8,128)} fusion(bf16[1024,7424]{1,0:T(8,128)(2,1)} %all-gather.2.cloned.1.call-done, bf16[1024,480]{1,0:T(8,128)(2,1)S(1)} %bitcast.206), kind=kOutput, calls=%fused_computation.16 | convolution fusion | flops 117440512 | bytes 1277952 | tf_op jit(solution)/shard_map/dot_general | solution.py:67
  149.7 12.3 %fusion.4 = f32[1,256,7168]{2,1,0:T(8,128)} fusion(bf16[1024,7424]{1,0:T(8,128)(2,1)} %all-gather.2.cloned.1.call-done, bf16[1024,480]{1,0:T(8,128)(2,1)S(1)} %bitcast.207), kind=kOutput, calls=%fused_computation.4 | convolution fusion | flops 3758096384 | bytes 22544384 | tf_op jit(solution)/shard_map/dot_general | solution.py:64
  162.0 0.7 all-to-all-done
  162.7 0.1 convert_element_type.17
  162.8 0.1 add_convert_fusion
  163.0 0.1 add_convert_fusion.1
  163.1 0.1 add_convert_fusion.2
  163.3 0.1 add_convert_fusion.3
  163.5 0.9 copy.38
  (12 shorter events, 0.2 us)
Async XLA Ops:
  7.2 125.7 %all-gather.2.cloned.1.call-start = ((), (), s32[]{:S(2)}) async-start(), calls=%async_computation.2 | async-start | bytes 15679488 | tf_op jit(solution)/shard_map/all_gather | solution.py:28
  18.8 125.2 %all-to-all-start.1 = ((bf16[32,32,480]{2,1,0:T(8,128)(2,1)}), bf16[32,32,480]{2,1,0:T(8,128)(2,1)S(1)}, u32[]{:S(2)}, u32[]{:S(2)}) async-start(bf16[32,32,480]{2,1,0:T(8,128)(2,1)} %pad_maximum_fusion), calls=%async_computation.1 | async-start | bytes 2097152 | tf_op jit(solution)/shard_map/all_to_all | solution.py:46
  144.0 18.8 %all-to-all-start = ((bf16[8,32,1024]{2,1,0:T(8,128)(2,1)}), bf16[8,32,1024]{2,1,0:T(8,128)(2,1)S(1)}, u32[]{:S(2)}, u32[]{:S(2)}) async-start(bf16[8,32,1024]{2,1,0:T(8,128)(2,1)} %bitcast.3), calls=%async_computation | async-start | bytes 1048576 | tf_op jit(solution)/shard_map/all_to_all | solution.py:57
Sparse Core Ops, SparseCore 0:
  10.8 122.0 all-gather.1

commit v2 on v1

--- a/solution.py
+++ b/solution.py
@@ -1,9 +1,150 @@
+import functools
+import itertools
+
 import jax
 import jax.numpy as jnp
 from jax import lax
+from jax.experimental import pallas as pl
+from jax.experimental.pallas import tpu as pltpu
 from jax.sharding import PartitionSpec as P
 
 BOTH = ("dp", "expert")
+MESH = pl.DeviceIdType.MESH
+
+
+def gather_kernel(
+    n_dp, n_group, chunks, x_ref, out_ref, send_sem, recv_sem, give_sem, take_sem, own_sem
+):
+    n_col, n_low = n_group // 2, 2
+    n_high = n_dp // n_low
+    swap = n_high == n_low
+    dp, group = lax.axis_index("dp"), lax.axis_index("expert")
+    col, core = group // 2, group % 2
+    high, low = dp // n_low, dp % n_low
+    sizes = (n_col, n_low, n_high)
+    rows = x_ref.shape[0]
+    part = rows // chunks
+
+    def moved(step, sign):
+        col_step, first, second = step
+        if swap:
+            low_step = first * (1 - core) + second * core
+            high_step = first * core + second * (1 - core)
+        else:
+            low_step, high_step = first, second
+        to_col = (col + sign * col_step + n_col) % n_col
+        to_low = (low + sign * low_step + n_low) % n_low
+        to_high = (high + sign * high_step + n_high) % n_high
+        return to_high * n_low + to_low, to_col * 2 + core
+
+    def row_span(at_dp, at_group, chunk):
+        start = (at_dp * n_group + at_group) * rows + chunk * part
+        return out_ref.at[pl.ds(pl.multiple_of(start, part), part)]
+
+    def flat(step, chunk):
+        return ((step[0] * sizes[1] + step[1]) * sizes[2] + step[2]) * chunks + chunk
+
+    def children(step):
+        last = max([i for i in range(3) if step[i]], default=-1)
+        for dim in range(last + 1, 3):
+            for hop in range(1, sizes[dim]):
+                yield tuple(hop if i == dim else 0 for i in range(3))
+
+    def source(step, chunk):
+        if not any(step):
+            return x_ref.at[pl.ds(chunk * part, part)]
+        return row_span(*moved(step, -1), chunk)
+
+    def forward(step, hop, chunk):
+        after = tuple(a + b for a, b in zip(step, hop))
+        return pltpu.make_async_remote_copy(
+            src_ref=source(step, chunk),
+            dst_ref=row_span(*moved(step, -1), chunk),
+            send_sem=send_sem.at[flat(after, chunk)],
+            recv_sem=recv_sem.at[flat(after, chunk)],
+            device_id=moved(hop, 1),
+            device_id_type=MESH,
+        )
+
+    def give(step, chunk):
+        return pltpu.make_async_remote_copy(
+            src_ref=source(step, chunk),
+            dst_ref=row_span(*moved(step, -1), chunk),
+            send_sem=give_sem.at[flat(step, chunk)],
+            recv_sem=take_sem.at[flat(step, chunk)],
+            device_id=(dp, col * 2 + 1 - core),
+            device_id_type=MESH,
+        )
+
+    def arrival(span, sem):
+        return pltpu.make_async_remote_copy(
+            src_ref=span,
+            dst_ref=span,
+            send_sem=give_sem.at[0],
+            recv_sem=sem,
+            device_id=(dp, col * 2 + 1 - core),
+            device_id_type=MESH,
+        )
+
+    start = (0, 0, 0)
+    hops = list(children(start))
+    barrier = pltpu.get_barrier_semaphore()
+    for hop in hops:
+        pl.semaphore_signal(barrier, inc=1, device_id=moved(hop, 1), device_id_type=MESH)
+    pl.semaphore_signal(
+        barrier, inc=1, device_id=(dp, col * 2 + 1 - core), device_id_type=MESH
+    )
+    pl.semaphore_wait(barrier, len(hops) + 1)
+
+    def when(event):
+        step, chunk = event
+        return (1.35 * step[0] + (step[1] > 0) + 1.2 * (step[2] > 0) + 0.5 * chunk, event)
+
+    events = sorted(
+        itertools.product(itertools.product(*[range(n) for n in sizes]), range(chunks)), key=when
+    )
+    own = pltpu.make_async_copy(
+        x_ref, out_ref.at[pl.ds((dp * n_group + group) * rows, rows)], own_sem
+    )
+    sent = []
+    for step, chunk in events:
+        if any(step):
+            arrival(row_span(*moved(step, -1), chunk), recv_sem.at[flat(step, chunk)]).wait_recv()
+        for hop in children(step):
+            copy = forward(step, hop, chunk)
+            copy.start()
+            sent.append(copy)
+        copy = give(step, chunk)
+        copy.start()
+        sent.append(copy)
+    own.start()
+    for step, chunk in events:
+        from_dp, from_group = moved((step[0], step[2], step[1]) if swap else step, -1)
+        span = row_span(from_dp, from_group + 1 - 2 * core, chunk)
+        arrival(span, take_sem.at[flat(step, chunk)]).wait_recv()
+    for copy in sent:
+        copy.wait_send()
+    own.wait()
+
+
+def gather_rows(x):
+    n_dp, n_group = lax.axis_size("dp"), lax.axis_size("expert")
+    chunks = 2 if x.shape[0] % 32 == 0 else 1
+    shards = n_dp * n_group // 2
+    full = jax.ShapeDtypeStruct((n_dp * n_group * x.shape[0], x.shape[1]), x.dtype)
+    sems = pltpu.SemaphoreType.DMA((shards * chunks,))
+    return pl.pallas_call(
+        functools.partial(gather_kernel, n_dp, n_group, chunks),
+        out_shape=full,
+        in_specs=[pl.BlockSpec(memory_space=pl.ANY)],
+        out_specs=pl.BlockSpec(memory_space=pl.ANY),
+        scratch_shapes=[sems, sems, sems, sems, pltpu.SemaphoreType.DMA],
+        compiler_params=pltpu.CompilerParams(collective_id=0, has_side_effects=True),
+        cost_estimate=pl.CostEstimate(
+            flops=0, bytes_accessed=8 * full.size * x.dtype.itemsize, transcendentals=0
+        ),
+        name="gather_rows",
+    )(x)
 
 
 def on_device(
@@ -25,11 +166,6 @@
     owned_units = hidden_units // n_dp
     is_live = jnp.arange(tok_rows, dtype=jnp.int32) < live_tokens[0]
     masked_grad = jnp.where(is_live[:, None], latent_grad, jnp.zeros_like(latent_grad))
-    everyone = lax.all_gather(
-        jnp.concatenate([output_grad, masked_grad], axis=1), BOTH, axis=0, tiled=True
-    )
-    all_grad = everyone[:, :model_width]
-    all_latent = everyone[:, model_width:]
     ids_at = expert_ids[:, :, None] == jnp.arange(expert_home.shape[0], dtype=jnp.int32)
     home = jnp.sum(jnp.where(ids_at, expert_home, 0), axis=2)
     scale = jnp.where(is_live[:, None], gate_weights, 0.0)
@@ -43,6 +179,12 @@
     by_owner = by_owner.reshape(n_dp * n_group, tok_rows, owned_units)
     dense_cut = dense_input.reshape(tok_rows, n_dp * n_group, -1).transpose(1, 0, 2)
     sent = jnp.concatenate([by_owner, dense_cut], axis=2)
+    sent, grads = lax.optimization_barrier(
+        (sent, jnp.concatenate([output_grad, masked_grad], axis=1))
+    )
+    everyone = gather_rows(grads)
+    all_grad = everyone[:, :model_width]
+    all_latent = everyone[:, model_width:]
     got = lax.all_to_all(sent, BOTH, split_axis=0, concat_axis=0, tiled=True)
     got = got.reshape(n_dp * n_group * tok_rows, -1)
     my_hidden = got[:, :owned_units]

time: 172 us -> 186 us (1.081)
  Pallas kernels: 0 us -> 86.9 us
  waiting for transfers between devices: 107 us -> 25.6 us
  blocking collectives: 0 us -> 32 us
  between operations: 14.9 us -> 1.48 us
  starting transfers between devices: 11 us -> 2.83 us
    all_gather x1 -> x0, waiting for transfers between devices: 107 us -> none  [on_device(): lax.all_gather(jnp.concatenate([output_grad, masked_grad], axis=1), BOTH,...]
    pallas_call x0 -> x1, Pallas kernels: none -> 86.9 us  [gather_rows(): pl.pallas_call(functools.partial(gather_kernel, n_dp, n_group, chunks), o...]
    all_to_all x0 -> x1, blocking collectives: none -> 32 us  [on_device(): lax.all_to_all(product.reshape(n_group, tok_rows, hidden_units), 'expert'...]
    all_to_all x1, waiting for transfers between devices: 0.01 us -> 25.6 us  [on_device(): got = lax.all_to_all(sent, BOTH, split_axis=0, concat_axis=0, tiled=True)]
    all_to_all x1, starting transfers between devices: 7.33 us -> 2.83 us  [on_device(): got = lax.all_to_all(sent, BOTH, split_axis=0, concat_axis=0, tiled=True)]
    all_to_all x1 -> x0, starting transfers between devices: 3.67 us -> none  [on_device(): lax.all_to_all(product.reshape(n_group, tok_rows, hidden_units), 'expert'...]
  transfers between devices with their start and end apart: 3 -> 1, of which waited for: 2 -> 1; matrix products, arithmetic and copies ran while one was open for 20% -> 1% of each run, Pallas kernels for 0% -> 0%
where the time goes in v2:
time: 186 us
  Pallas kernels  86.9 us (47%)
  blocking collectives  32 us (17%)
  waiting for transfers between devices  25.6 us (14%)
  matrix products  24.6 us (13%)
  other arithmetic  7.67 us (4%)
  local copies, waits for them, and re-layouts  4.76 us (3%)
  starting transfers between devices  2.83 us (2%)
    pallas_call x1, Pallas kernels, gather_rows(): pl.pallas_call(functools.partial(gather_kernel, n_dp, n_group, chunks), o...  86.9 us
    all_to_all x1, blocking collectives, on_device(): lax.all_to_all(product.reshape(n_group, tok_rows, hidden_units), 'expert'...  32 us
    all_to_all x1, waiting for transfers between devices, on_device(): got = lax.all_to_all(sent, BOTH, split_axis=0, concat_axis=0, tiled=True)  25.6 us
    dot_general x1, matrix products, on_device(): lax.dot_general(my_hidden, all_grad, (((0,), (0,)), ((), ())), preferred_...  12.3 us
    dot_general x1, matrix products, on_device(): lax.dot_general(my_replica, down_weight[0], (((1,), (1,)), ((), ())), pre...  10.3 us
  transfers between devices with their start and end apart: 1, of which 1 were waited for; matrix products, arithmetic and copies ran while one was open for 1% of the time, Pallas kernels for 0%

profile of v2, /device:TPU:0, one launch (start us, length us, event | category | flops | bytes accessed | tf_op | source)
XLA Modules:
  0.0 185.8 jit_solution(10882394211205640290)
XLA Ops:
  1.3 0.7 broadcast_select_fusion.1
  2.0 0.8 select_reduce_fusion
  2.8 1.0 convert_element_type.16
  3.8 1.4 slice_reduce_fusion.3
  5.2 0.1 mul.656
  5.3 0.1 mul.664
  5.4 0.1 mul.672
  5.5 0.1 mul.680
  5.6 1.8 reshape.1380
  7.4 0.3 copy.37
  7.7 0.8 broadcast_select_fusion
  8.5 0.7 fusion.14
  9.2 1.1 pad_maximum_fusion
  10.3 1.8 pad_maximum_fusion.1.x_ref
  12.2 86.9 %gather_rows.1 = bf16[1024,7424]{1,0:T(8,128)(2,1)} custom-call(bf16[32,7424]{1,0:T(8,128)(2,1)} %pad_maximum_fusion.1.x_ref), custom_call_target="tpu_custom_call" | custom-call | bytes 121634816 | tf_op jit(solution)/shard_map/gather_rows/pallas_call | solution.py:136
  99.1 10.3 %fusion.8 = bf16[256,1024]{1,0:T(8,128)(2,1)S(1)} fusion(bf16[1,1024,7168]{2,1,0:T(8,128)(2,1)} %param.15, bf16[1024,7424]{1,0:T(8,128)(2,1)} %gather_rows.1, s32[]{:T(128)S(6)} %select_n.23), kind=kOutput, calls=%fused_computation.6 | convolution fusion | flops 3758358528 | bytes 18874372 | tf_op jit(solution)/shard_map/dot_general | solution.py:196
  109.3 32.0 %all_to_all.10 = bf16[8,32,1024]{2,1,0:T(8,128)(2,1)S(1)} all-to-all(bf16[8,32,1024]{2,1,0:T(8,128)(2,1)S(1)} %bitcast.209), channel_id=1, replica_groups=mesh['dp'=4,'expert'=8] {'expert'}, dimensions={0} | all-to-all | bytes 1048576 | tf_op jit(solution)/shard_map/all_to_all | solution.py:199
  141.4 2.8 %all-to-all-start.1 = ((bf16[32,32,480]{2,1,0:T(8,128)(2,1)}), bf16[32,32,480]{2,1,0:T(8,128)(2,1)S(1)}, u32[]{:S(2)}, u32[]{:S(2)}) async-start(bf16[32,32,480]{2,1,0:T(8,128)(2,1)} %pad_maximum_fusion), calls=%async_computation.1 | async-start | bytes 2097152 | tf_op jit(solution)/shard_map/all_to_all | solution.py:188
  144.3 0.1 convert_element_type.19
  144.4 0.1 add_convert_fusion.3
  144.5 0.1 add_convert_fusion.2
  144.7 0.1 add_convert_fusion.1
  144.8 0.1 add_convert_fusion
  145.0 0.9 copy.38
  145.9 25.6 %all-to-all-done.1 = bf16[32,32,480]{2,1,0:T(8,128)(2,1)S(1)} async-done(((bf16[32,32,480]{2,1,0:T(8,128)(2,1)}), bf16[32,32,480]{2,1,0:T(8,128)(2,1)S(1)}, u32[]{:S(2)}, u32[]{:S(2)}) %all-to-all-start.1) | async-done | bytes 983072 | tf_op jit(solution)/shard_map/all_to_all | solution.py:188
  171.5 12.3 %fusion.4 = f32[1,256,7168]{2,1,0:T(8,128)} fusion(bf16[1024,7424]{1,0:T(8,128)(2,1)} %gather_rows.1, bf16[1024,480]{1,0:T(8,128)(2,1)S(1)} %bitcast.206), kind=kOutput, calls=%fused_computation.4 | convolution fusion | flops 3758096384 | bytes 22544384 | tf_op jit(solution)/shard_map/dot_general | solution.py:206
  183.8 2.1 %fusion.17 = f32[224,256]{1,0:T(8,128)} fusion(bf16[1024,480]{1,0:T(8,128)(2,1)S(1)} %bitcast.207, bf16[1024,7424]{1,0:T(8,128)(2,1)} %gather_rows.1), kind=kOutput, calls=%fused_computation.16 | convolution fusion | flops 117440512 | bytes 1277952 | tf_op jit(solution)/shard_map/dot_general | solution.py:209
  (12 shorter events, 0.2 us)
Async XLA Ops:
  141.4 30.1 %all-to-all-start.1 = ((bf16[32,32,480]{2,1,0:T(8,128)(2,1)}), bf16[32,32,480]{2,1,0:T(8,128)(2,1)S(1)}, u32[]{:S(2)}, u32[]{:S(2)}) async-start(bf16[32,32,480]{2,1,0:T(8,128)(2,1)} %pad_maximum_fusion), calls=%async_computation.1 | async-start | bytes 2097152 | tf_op jit(solution)/shard_map/all_to_all | solution.py:188

commit v3 on v2

--- a/solution.py
+++ b/solution.py
@@ -13,7 +13,20 @@
 
 
 def gather_kernel(
-    n_dp, n_group, chunks, x_ref, out_ref, send_sem, recv_sem, give_sem, take_sem, own_sem
+    n_dp,
+    n_group,
+    chunks,
+    x_ref,
+    swap_ref,
+    out_ref,
+    got_ref,
+    send_sem,
+    recv_sem,
+    give_sem,
+    take_sem,
+    post_sem,
+    mail_sem,
+    own_sem,
 ):
     n_col, n_low = n_group // 2, 2
     n_high = n_dp // n_low
@@ -32,7 +45,12 @@
             high_step = first * core + second * (1 - core)
         else:
             low_step, high_step = first, second
-        to_col = (col + sign * col_step + n_col) % n_col
+        if n_col & (n_col - 1):
+            to_col = (col + sign * col_step + n_col) % n_col
+        else:
+            to_col = 0
+            for bit in range(n_col.bit_length() - 1):
+                to_col += (col // 2**bit + (col_step >> bit)) % 2 * 2**bit
         to_low = (low + sign * low_step + n_low) % n_low
         to_high = (high + sign * high_step + n_high) % n_high
         return to_high * n_low + to_low, to_col * 2 + core
@@ -86,15 +104,33 @@
             device_id_type=MESH,
         )
 
-    start = (0, 0, 0)
-    hops = list(children(start))
+    me, n_all = dp * n_group + group, n_dp * n_group
+
+    def there(hop):
+        return (me + hop) % n_all
+
+    def post(hop):
+        return pltpu.make_async_remote_copy(
+            src_ref=swap_ref.at[there(hop)],
+            dst_ref=got_ref.at[me],
+            send_sem=post_sem.at[hop],
+            recv_sem=mail_sem.at[hop],
+            device_id=(there(hop) // n_group, there(hop) % n_group),
+            device_id_type=MESH,
+        )
+
     barrier = pltpu.get_barrier_semaphore()
-    for hop in hops:
-        pl.semaphore_signal(barrier, inc=1, device_id=moved(hop, 1), device_id_type=MESH)
-    pl.semaphore_signal(
-        barrier, inc=1, device_id=(dp, col * 2 + 1 - core), device_id_type=MESH
-    )
-    pl.semaphore_wait(barrier, len(hops) + 1)
+
+    @pl.loop(1, n_all)
+    def _(hop):
+        pl.semaphore_signal(
+            barrier,
+            inc=1,
+            device_id=(there(hop) // n_group, there(hop) % n_group),
+            device_id_type=MESH,
+        )
+
+    pl.semaphore_wait(barrier, n_all - 1)
 
     def when(event):
         step, chunk = event
@@ -103,11 +139,18 @@
     events = sorted(
         itertools.product(itertools.product(*[range(n) for n in sizes]), range(chunks)), key=when
     )
-    own = pltpu.make_async_copy(
-        x_ref, out_ref.at[pl.ds((dp * n_group + group) * rows, rows)], own_sem
-    )
+    own = pltpu.make_async_copy(x_ref, out_ref.at[pl.ds(me * rows, rows)], own_sem.at[0])
+    kept = pltpu.make_async_copy(swap_ref.at[me], got_ref.at[me], own_sem.at[1])
     sent = []
-    for step, chunk in events:
+    for place, (step, chunk) in enumerate(events):
+        if place == chunks:
+
+            @pl.loop(1, n_all)
+            def _(hop):
+                post(hop).start()
+
+            own.start()
+            kept.start()
         if any(step):
             arrival(row_span(*moved(step, -1), chunk), recv_sem.at[flat(step, chunk)]).wait_recv()
         for hop in children(step):
@@ -117,34 +160,50 @@
         copy = give(step, chunk)
         copy.start()
         sent.append(copy)
-    own.start()
     for step, chunk in events:
         from_dp, from_group = moved((step[0], step[2], step[1]) if swap else step, -1)
         span = row_span(from_dp, from_group + 1 - 2 * core, chunk)
         arrival(span, take_sem.at[flat(step, chunk)]).wait_recv()
     for copy in sent:
         copy.wait_send()
+
+    @pl.loop(1, n_all)
+    def _(hop):
+        post(hop).wait_send()
+        arrival(got_ref.at[(me + n_all - hop) % n_all], mail_sem.at[hop]).wait_recv()
+
     own.wait()
-
-
-def gather_rows(x):
+    kept.wait()
+
+
+def gather_and_swap(x, blocks):
     n_dp, n_group = lax.axis_size("dp"), lax.axis_size("expert")
     chunks = 2 if x.shape[0] % 32 == 0 else 1
     shards = n_dp * n_group // 2
     full = jax.ShapeDtypeStruct((n_dp * n_group * x.shape[0], x.shape[1]), x.dtype)
     sems = pltpu.SemaphoreType.DMA((shards * chunks,))
+    mail_sems = pltpu.SemaphoreType.DMA((n_dp * n_group,))
+    anywhere = pl.BlockSpec(memory_space=pl.ANY)
     return pl.pallas_call(
         functools.partial(gather_kernel, n_dp, n_group, chunks),
-        out_shape=full,
-        in_specs=[pl.BlockSpec(memory_space=pl.ANY)],
-        out_specs=pl.BlockSpec(memory_space=pl.ANY),
-        scratch_shapes=[sems, sems, sems, sems, pltpu.SemaphoreType.DMA],
+        out_shape=(full, jax.ShapeDtypeStruct(blocks.shape, blocks.dtype)),
+        in_specs=[anywhere, anywhere],
+        out_specs=(anywhere, anywhere),
+        scratch_shapes=[
+            sems,
+            sems,
+            sems,
+            sems,
+            mail_sems,
+            mail_sems,
+            pltpu.SemaphoreType.DMA((2,)),
+        ],
         compiler_params=pltpu.CompilerParams(collective_id=0, has_side_effects=True),
         cost_estimate=pl.CostEstimate(
             flops=0, bytes_accessed=8 * full.size * x.dtype.itemsize, transcendentals=0
         ),
-        name="gather_rows",
-    )(x)
+        name="gather_and_swap",
+    )(x, blocks)
 
 
 def on_device(
@@ -179,13 +238,10 @@
     by_owner = by_owner.reshape(n_dp * n_group, tok_rows, owned_units)
     dense_cut = dense_input.reshape(tok_rows, n_dp * n_group, -1).transpose(1, 0, 2)
     sent = jnp.concatenate([by_owner, dense_cut], axis=2)
-    sent, grads = lax.optimization_barrier(
-        (sent, jnp.concatenate([output_grad, masked_grad], axis=1))
-    )
-    everyone = gather_rows(grads)
+    grads = jnp.concatenate([output_grad, masked_grad], axis=1)
+    everyone, got = gather_and_swap(grads, sent)
     all_grad = everyone[:, :model_width]
     all_latent = everyone[:, model_width:]
-    got = lax.all_to_all(sent, BOTH, split_axis=0, concat_axis=0, tiled=True)
     got = got.reshape(n_dp * n_group * tok_rows, -1)
     my_hidden = got[:, :owned_units]
     my_dense = got[:, owned_units:]

time: 186 us -> 133 us (0.72)
  blocking collectives: 32 us -> 0 us
  waiting for transfers between devices: 25.6 us -> 0.71 us
  Pallas kernels: 86.9 us -> 88.8 us
    all_to_all x1 -> x0, blocking collectives: 32 us -> none  [on_device(): lax.all_to_all(product.reshape(n_group, tok_rows, hidden_units), 'expert'...]
    all_to_all x1, waiting for transfers between devices: 25.6 us -> 0.71 us  [on_device(): lax.all_to_all(product.reshape(n_group, tok_rows, hidden_units), 'expert'...]
    pallas_call x1, Pallas kernels: 86.9 us -> 88.8 us  [gather_and_swap(): pl.pallas_call(functools.partial(gather_kernel, n_dp, n_group, chunks), o...]
  transfers between devices with their start and end apart: 1 -> 1, of which waited for: 1 -> 1; matrix products, arithmetic and copies ran while one was open for 1% -> 11% of each run, Pallas kernels for 0% -> 0%
where the time goes in v3:
time: 133 us
  Pallas kernels  88.8 us (67%)
  matrix products  25.5 us (19%)
  other arithmetic  7.67 us (6%)
  local copies, waits for them, and re-layouts  4.76 us (4%)
  starting transfers between devices  3.67 us (3%)
  between operations  1.49 us (1%)
    pallas_call x1, Pallas kernels, gather_and_swap(): pl.pallas_call(functools.partial(gather_kernel, n_dp, n_group, chunks), o...  88.8 us
    dot_general x1, matrix products, on_device(): lax.dot_general(my_hidden, all_grad, (((0,), (0,)), ((), ())), preferred_...  12.3 us
    dot_general x1, matrix products, on_device(): lax.dot_general(my_replica, down_weight[0], (((1,), (1,)), ((), ())), pre...  11.1 us
    all_to_all x1, starting transfers between devices, on_device(): lax.all_to_all(product.reshape(n_group, tok_rows, hidden_units), 'expert'...  3.67 us
  transfers between devices with their start and end apart: 1, of which 1 were waited for; matrix products, arithmetic and copies ran while one was open for 11% of the time, Pallas kernels for 0%

profile of v3, /device:TPU:0, one launch (start us, length us, event | category | flops | bytes accessed | tf_op | source)
XLA Modules:
  0.0 132.6 jit_solution(714251753903065654)
XLA Ops:
  1.3 0.7 broadcast_select_fusion.1
  2.0 0.8 select_reduce_fusion
  2.8 1.0 convert_element_type.16
  3.8 1.4 %slice_reduce_fusion.3 = (f32[32,1024]{1,0:T(8,128)S(1)}, f32[32,1024]{1,0:T(8,128)S(1)}, f32[32,1024]{1,0:T(8,128)S(1)}, f32[32,1024]{1,0:T(8,128)S(1)}) fusion(f32[32,4,1024]{2,1,0:T(4,128)S(1)} %convert_element_type.16), kind=kLoop, calls=%fused_computation.34 | loop fusion | bytes 1048576 | tf_op jit(solution)/shard_map/slice | solution.py:235
  5.2 0.1 mul.656
  5.3 0.1 mul.664
  5.4 0.1 mul.672
  5.5 0.1 mul.680
  5.6 1.8 %reshape.1380 = bf16[32,32,224]{2,1,0:T(8,128)(2,1)S(1)} reshape(bf16[32,7168]{1,0:T(8,128)(2,1)} %param.16) | data formatting | bytes 917504 | tf_op jit(solution)/shard_map/reshape | solution.py:239
  7.4 0.3 copy.39
  7.7 0.8 broadcast_select_fusion
  8.5 0.7 fusion.14
  9.2 1.1 pad_maximum_fusion.swap_ref
  10.3 1.8 %pad_maximum_fusion.1.x_ref = bf16[32,7424]{1,0:T(8,128)(2,1)} fusion(bf16[32,256]{1,0:T(8,128)(2,1)S(1)} %broadcast_select_fusion, bf16[32,7168]{1,0:T(8,128)(2,1)} %param.13), kind=kLoop, calls=%fused_computation.21 | loop fusion | flops 950272 | bytes 950272 | tf_op jit(solution)/shard_map/concatenate | solution.py:241
  12.2 88.8 %gather_and_swap.1 = (bf16[1024,7424]{1,0:T(8,128)(2,1)}, bf16[32,32,480]{2,1,0:T(8,128)(2,1)}) custom-call(bf16[32,7424]{1,0:T(8,128)(2,1)} %pad_maximum_fusion.1.x_ref, bf16[32,32,480]{2,1,0:T(8,128)(2,1)} %pad_maximum_fusion.swap_ref), custom_call_target="tpu_custom_call" | custom-call | bytes 121634816 | tf_op jit(solution)/shard_map/gather_and_swap/pallas_call | solution.py:187
  101.0 0.0 copy-start
  101.0 11.1 %fusion.8 = bf16[256,1024]{1,0:T(8,128)(2,1)} fusion(bf16[1,1024,7168]{2,1,0:T(8,128)(2,1)} %param.15, bf16[1024,7424]{1,0:T(8,128)(2,1)} %get-tuple-element.5, s32[]{:T(128)S(6)} %select_n.23), kind=kOutput, calls=%fused_computation.6 | convolution fusion | flops 3758358528 | bytes 18874372 | tf_op jit(solution)/shard_map/dot_general | solution.py:252
  112.2 3.7 %all-to-all-start = ((bf16[8,32,1024]{2,1,0:T(8,128)(2,1)}), bf16[8,32,1024]{2,1,0:T(8,128)(2,1)S(1)}, u32[]{:S(2)}, u32[]{:S(2)}) async-start(bf16[8,32,1024]{2,1,0:T(8,128)(2,1)} %bitcast.24), calls=%async_computation | async-start | bytes 1048576 | tf_op jit(solution)/shard_map/all_to_all | solution.py:255
  115.9 0.0 copy-done
  115.9 2.1 %fusion.17 = f32[224,256]{1,0:T(8,128)} fusion(bf16[1024,480]{1,0:T(8,128)(2,1)S(1)} %bitcast.213, bf16[1024,7424]{1,0:T(8,128)(2,1)} %get-tuple-element.5), kind=kOutput, calls=%fused_computation.16 | convolution fusion | flops 117440512 | bytes 1277952 | tf_op jit(solution)/shard_map/dot_general | solution.py:265
  118.0 12.3 %fusion.4 = f32[1,256,7168]{2,1,0:T(8,128)} fusion(bf16[1024,7424]{1,0:T(8,128)(2,1)} %get-tuple-element.5, bf16[1024,480]{1,0:T(8,128)(2,1)S(1)} %bitcast.214), kind=kOutput, calls=%fused_computation.4 | convolution fusion | flops 3758096384 | bytes 22544384 | tf_op jit(solution)/shard_map/dot_general | solution.py:262
  130.2 0.7 all-to-all-done
  130.9 0.1 convert_element_type.19
  131.1 0.1 add_convert_fusion.3
  131.2 0.1 add_convert_fusion.2
  131.4 0.1 add_convert_fusion.1
  131.5 0.1 add_convert_fusion
  131.7 0.9 copy.37
  (12 shorter events, 0.2 us)
Async XLA Ops:
  101.0 14.9 %copy-start = (bf16[32,32,480]{2,1,0:T(8,128)(2,1)S(1)}, bf16[32,32,480]{2,1,0:T(8,128)(2,1)}, u32[]{:S(2)}) copy-start(bf16[32,32,480]{2,1,0:T(8,128)(2,1)} %get-tuple-element.6) | copy-start | bytes 2949124
  112.2 18.8 %all-to-all-start = ((bf16[8,32,1024]{2,1,0:T(8,128)(2,1)}), bf16[8,32,1024]{2,1,0:T(8,128)(2,1)S(1)}, u32[]{:S(2)}, u32[]{:S(2)}) async-start(bf16[8,32,1024]{2,1,0:T(8,128)(2,1)} %bitcast.24), calls=%async_computation | async-start | bytes 1048576 | tf_op jit(solution)/shard_map/all_to_all | solution.py:255
